TPU v7x, 32 devices: a whole 2x2x4 slice. The times are simulated.
32 devices in a mesh: gx: 4 (over x, core), gy: 4 (over z), gz: 2 (over y).
Axes of the slice: x: 2, y: 2, z: 4, core: 2. Of those that a mesh axis runs over, the one named last changes fastest.
Arguments:
- kappa: float32 [5, 5, 5, 4, 4, 128], P(None, None, None, 'gx', 'gy', 'gz'), may hold values from 0.2 to 5
- source: float32 [5, 5, 5, 4, 4, 128], P(None, None, None, 'gx', 'gy', 'gz'), may hold values from -24 to 24
Outputs:
- solution: float32 [16, 16, 512], P('gx', 'gy', 'gz')
- residual: float32 [16, 16, 512], P('gx', 'gy', 'gz')
All inputs are finite; a program needn't handle non-finite values.
Results may differ from a plain program's by a relative error of at most 0.0003.
Values sent between devices are 32-bit elements; how exact they have to be, the bound alone decides.
A program may use at most 64 MiB of HBM per device.

v0:
```python
import math
import jax
import jax.numpy as jnp
import numpy as np
from jax import lax
from jax.sharding import PartitionSpec as P

LEVELS = 3
relax_weight = 0.6


def extended(cells, sides, width):
    for axis, dim in sides:
        count = lax.axis_size(axis)
        ends = count - 1
        head = lax.slice_in_dim(cells, 0, width, axis=dim)
        tail = lax.slice_in_dim(cells, cells.shape[dim] - width, cells.shape[dim], axis=dim)
        cells = jnp.concatenate(
            [
                lax.ppermute(tail, axis, [(i, (i + 1) % count) for i in range(ends)]),
                cells,
                lax.ppermute(head, axis, [((i + 1) % count, i) for i in range(ends)]),
            ],
            axis=dim,
        )
    return cells


def gll_tables():
    points = np.array([-1.0, -math.sqrt(3.0 / 7.0), 0.0, math.sqrt(3.0 / 7.0), 1.0])
    quad_weights = np.array([0.1, 49.0 / 90.0, 32.0 / 45.0, 49.0 / 90.0, 0.1])
    bary = np.array(
        [np.prod([points[i] - points[k] for k in range(5) if k != i]) for i in range(5)]
    )
    deriv = np.zeros((5, 5))
    for i in range(5):
        for j in range(5):
            if i != j:
                deriv[i, j] = bary[i] / (bary[j] * (points[i] - points[j]))
    for i in range(5):
        deriv[i, i] = -np.sum(deriv[i])
    return (
        jnp.asarray(points, jnp.float32),
        jnp.asarray(quad_weights, jnp.float32),
        jnp.asarray(deriv, jnp.float32),
    )


def split_first(values):
    count = (values.shape[0] - 1) // 4
    lower = jnp.swapaxes(values[:-1].reshape((count, 4) + values.shape[1:]), 0, 1)
    return jnp.concatenate([lower, values[4::4][None]], axis=0)


def merge_first(block):
    count = block.shape[1]
    rest = block.shape[2:]
    lower = jnp.swapaxes(block[:4], 0, 1).reshape((4 * count,) + rest)
    tail = jnp.concatenate([jnp.zeros((count, 3) + rest, block.dtype), block[4][:, None]], axis=1)
    tail = tail.reshape((4 * count,) + rest)
    spare = [(0, 0)] * len(rest)
    return jnp.pad(lower, [(0, 1)] + spare) + jnp.pad(tail, [(1, 0)] + spare)


def element_view(field):
    element_portion = split_first(field)
    element_portion = split_first(jnp.moveaxis(element_portion, 2, 0))
    element_portion = split_first(jnp.moveaxis(element_portion, 4, 0))
    return jnp.transpose(element_portion, (4, 2, 0, 5, 3, 1))


def node_sum(block):
    element_portion = jnp.transpose(block, (2, 5, 1, 4, 0, 3))
    element_portion = jnp.moveaxis(merge_first(element_portion), 0, 4)
    element_portion = jnp.moveaxis(merge_first(element_portion), 0, 2)
    return merge_first(element_portion)


def stiffness_terms(field, weighted, deriv):
    highest = lax.Precision.HIGHEST
    local = element_view(field)
    grad_x = jnp.einsum("ia,abcxyz->ibcxyz", deriv, local, precision=highest)
    grad_y = jnp.einsum("jb,abcxyz->ajcxyz", deriv, local, precision=highest)
    grad_z = jnp.einsum("kc,abcxyz->abkxyz", deriv, local, precision=highest)
    back = jnp.einsum("ia,ibcxyz->abcxyz", deriv, weighted * grad_x, precision=highest)
    back = back + jnp.einsum("jb,ajcxyz->abcxyz", deriv, weighted * grad_y, precision=highest)
    back = back + jnp.einsum("kc,abkxyz->abcxyz", deriv, weighted * grad_z, precision=highest)
    return node_sum(back)


def mass_pair(paired, width):
    return jnp.stack(
        [width / 6.0 * (2.0 * paired[0] + paired[1]), width / 6.0 * (paired[0] + 2.0 * paired[1])]
    )


def stiff_pair(paired, width):
    slope = (paired[0] - paired[1]) / width
    return jnp.stack([slope, -slope])


def lor_terms(field, coeff, spacing):
    width_x, width_y, width_z = spacing
    zpairs = jnp.stack([field[:, :, :-1], field[:, :, 1:]])
    zmass = mass_pair(zpairs, width_z)
    stiffness_along_z = stiff_pair(zpairs, width_z)
    ymass = jnp.stack([zmass[:, :, :-1], zmass[:, :, 1:]])
    ystiff = jnp.stack([stiffness_along_z[:, :, :-1], stiffness_along_z[:, :, 1:]])
    column_y = width_y[:, None]
    first = mass_pair(ymass, column_y)
    second = stiff_pair(ymass, column_y) + mass_pair(ystiff, column_y)
    column_x = width_x[:, None, None]
    xfirst = jnp.stack([first[:, :, :-1], first[:, :, 1:]])
    xsecond = jnp.stack([second[:, :, :-1], second[:, :, 1:]])
    cells = (stiff_pair(xfirst, column_x) + mass_pair(xsecond, column_x)) * coeff
    total = jnp.zeros(field.shape, jnp.float32)
    for a in range(2):
        for b in range(2):
            for c in range(2):
                total = total + jnp.pad(cells[a, b, c], ((a, 1 - a), (b, 1 - b), (c, 1 - c)))
    return total


def lor_diagonal(coeff, spacing):
    width_x = spacing[0][:, None, None]
    width_y = spacing[1][None, :, None]
    width_z = spacing[2][None, None, :]
    cells = coeff * (
        width_y * width_z / (9.0 * width_x)
        + width_x * width_z / (9.0 * width_y)
        + width_x * width_y / (9.0 * width_z)
    )
    shape = tuple((n + 1 for n in coeff.shape))
    total = jnp.zeros(shape, jnp.float32)
    for a in range(2):
        for b in range(2):
            for c in range(2):
                total = total + jnp.pad(cells, ((a, 1 - a), (b, 1 - b), (c, 1 - c)))
    return total


def subcell_coefficient(kappa):
    averaged = 0.5 * (kappa[:-1] + kappa[1:])
    averaged = 0.5 * (averaged[:, :-1] + averaged[:, 1:])
    averaged = 0.5 * (averaged[:, :, :-1] + averaged[:, :, 1:])
    count_x, count_y, count_z = averaged.shape[3:]
    return jnp.transpose(averaged, (3, 0, 4, 1, 5, 2)).reshape(
        4 * count_x, 4 * count_y, 4 * count_z
    )


def coarsen(coeff):
    nx, ny, nz = coeff.shape
    return jnp.mean(coeff.reshape(nx // 2, 2, ny // 2, 2, nz // 2, 2), axis=(1, 3, 5))


def interp_weights(width):
    paired = width.reshape(-1, 2)
    span = paired[:, 0] + paired[:, 1]
    return (paired[:, 1] / span, paired[:, 0] / span)


def prolong_first(coarse, left, right):
    shape = (-1,) + (1,) * (coarse.ndim - 1)
    middle = left.reshape(shape) * coarse[:-1] + right.reshape(shape) * coarse[1:]
    woven = jnp.stack([coarse[:-1], middle], axis=1).reshape(
        (2 * (coarse.shape[0] - 1),) + coarse.shape[1:]
    )
    return jnp.concatenate([woven, coarse[-1:]], axis=0)


def restrict_first(fine, left, right):
    shape = (-1,) + (1,) * (fine.ndim - 1)
    middle = fine[1::2]
    spare = [(0, 0)] * (fine.ndim - 1)
    return (
        fine[0::2]
        + jnp.pad(left.reshape(shape) * middle, [(0, 1)] + spare)
        + jnp.pad(right.reshape(shape) * middle, [(1, 0)] + spare)
    )


def prolong(coarse, weight_sets):
    for axis in range(3):
        left, right = weight_sets[axis]
        coarse = jnp.moveaxis(prolong_first(jnp.moveaxis(coarse, axis, 0), left, right), 0, axis)
    return coarse


def restrict(fine, weight_sets):
    for axis in range(3):
        left, right = weight_sets[axis]
        fine = jnp.moveaxis(restrict_first(jnp.moveaxis(fine, axis, 0), left, right), 0, axis)
    return fine


def collapse_leading(padded):
    inner = padded[1:-1]
    head = inner[0] + padded[0]
    tail = inner[-1] + padded[-1]
    return jnp.concatenate([head[None], inner[1:-1], tail[None]], axis=0)


def fold_axis(padded, axis):
    return jnp.moveaxis(collapse_leading(jnp.moveaxis(padded, axis, 0)), 0, axis)


def assemble(partial_value):
    padded = extended(partial_value, (("gx", 0), ("gy", 1), ("gz", 2)), 1)
    return fold_axis(fold_axis(fold_axis(padded, 0), 1), 2)


def side_mask(cells, position, devices):
    index = position * cells + jnp.arange(cells + 1)
    return ((index > 0) & (index < cells * devices)).astype(jnp.float32)


def block_mask(shape):
    mask_x = side_mask(shape[0], lax.axis_index("gx"), lax.axis_size("gx"))
    mask_y = side_mask(shape[1], lax.axis_index("gy"), lax.axis_size("gy"))
    mask_z = side_mask(shape[2], lax.axis_index("gz"), lax.axis_size("gz"))
    return mask_x[:, None, None] * mask_y[None, :, None] * mask_z[None, None, :]


def owned_mask(shape):
    sides = [(jnp.arange(n + 1) >= 1).astype(jnp.float32) for n in shape]
    return sides[0][:, None, None] * sides[1][None, :, None] * sides[2][None, None, :]


def cycle(level, forcing, levels):
    coeff, spacing, diag, mask, weight_sets, owned = levels[level]
    guess = relax_weight * forcing / diag
    if level == LEVELS - 1:
        guess = (
            guess
            + relax_weight * (forcing - mask * assemble(lor_terms(guess, coeff, spacing))) / diag
        )
        return guess
    defect = forcing * owned - lor_terms(guess, coeff, spacing)
    coarse = levels[level + 1][3] * assemble(restrict(defect, weight_sets))
    guess = guess + prolong(cycle(level + 1, coarse, levels), weight_sets)
    return (
        guess + relax_weight * (forcing - mask * assemble(lor_terms(guess, coeff, spacing))) / diag
    )


def inner_pair(resid, precond, image):
    local_rho = jnp.sum(resid[1:, 1:, 1:] * precond[1:, 1:, 1:])
    local_curv = jnp.sum(precond[1:, 1:, 1:] * image[1:, 1:, 1:])
    return lax.psum((local_rho, local_curv), ("gx", "gy", "gz"))


def body(kappa, source):
    points, quad_weights, deriv = gll_tables()
    cube = (
        quad_weights[:, None, None] * quad_weights[None, :, None] * quad_weights[None, None, :]
    ).reshape(5, 5, 5, 1, 1, 1)
    weighted = kappa * cube
    counts = kappa.shape[3:]
    finest_mask = block_mask([4 * c for c in counts])
    rhs = finest_mask * assemble(node_sum(cube * source))
    gaps = points[1:] - points[:-1]
    spacing = [jnp.tile(gaps, c) for c in counts]
    coeff = subcell_coefficient(kappa)
    levels = []
    for level in range(LEVELS):
        weight_sets = [interp_weights(h) for h in spacing] if level < LEVELS - 1 else None
        diag = assemble(lor_diagonal(coeff, spacing))
        levels.append(
            (coeff, spacing, diag, block_mask(coeff.shape), weight_sets, owned_mask(coeff.shape))
        )
        if level < LEVELS - 1:
            coeff = coarsen(coeff)
            spacing = [h.reshape(-1, 2).sum(axis=1) for h in spacing]

    def operator(field):
        return finest_mask * assemble(stiffness_terms(field, weighted, deriv))

    resid = rhs
    precond = cycle(0, resid, levels)
    image = operator(precond)
    rho_old, curv = inner_pair(resid, precond, image)
    alpha = rho_old / curv
    direction, along = (precond, image)
    iterate = alpha * direction
    resid = resid - alpha * along
    precond = cycle(0, resid, levels)
    image = operator(precond)
    rho_new, curv = inner_pair(resid, precond, image)
    ratio = rho_new / rho_old
    alpha = rho_new / (curv - ratio * rho_new / alpha)
    direction = precond + ratio * direction
    along = image + ratio * along
    iterate = iterate + alpha * direction
    resid = resid - alpha * along
    return (iterate[1:, 1:, 1:], resid[1:, 1:, 1:])


def solution(mesh):
    placed = (P(None, None, None, "gx", "gy", "gz"), P(None, None, None, "gx", "gy", "gz"))
    return jax.shard_map(
        body,
        mesh=mesh,
        in_specs=placed,
        out_specs=(P("gx", "gy", "gz"), P("gx", "gy", "gz")),
        check_vma=False,
    )
```

profile of v0, /device:TPU:14, one launch (start us, length us, event | category | flops | bytes accessed | tf_op | source)
XLA Modules:
  0.0 476.9 jit_solution(2688961487254693226)
XLA Ops:
  36.4 4.5 collective-permute-start.35
  51.3 4.5 collective-permute-start.23
  59.9 3.9 collective-permute-start.9
  65.8 3.9 collective-permute-start.3
  71.1 4.5 collective-permute-start.11
  77.0 4.5 collective-permute-start.5
  96.4 3.9 collective-permute-start.15
  103.3 4.5 collective-permute-start.17
  119.3 3.9 collective-permute-start.27
  126.2 4.5 collective-permute-start.29
  141.6 3.9 collective-permute-start.39
  148.5 4.5 collective-permute-start.41
  164.6 3.9 collective-permute-start.45
  171.4 4.5 collective-permute-start.47
  183.7 3.8 collective-permute-start.49
  190.9 3.9 collective-permute-start.51
  197.8 4.5 collective-permute-start.53
  221.2 3.9 collective-permute-start.57
  228.1 4.5 collective-permute-start.59
  235.6 42.7 %all-reduce.156 = (f32[]{:T(128)}, f32[]{:T(128)}) all-reduce(f32[]{:T(128)} %get-tuple-element.13, f32[]{:T(128)} %get-tuple-element.12), channel_id=1, replica_groups=mesh['gx'=4,'gy'=4,'gz'=2] {'gx','gy','gz'}, use_global_device_ids=true, to_apply=%region_6.7 | all-reduce | flops 2 | bytes 16 | tf_op jit(solution)/shard_map/psum | solution.py:250
  297.8 4.5 collective-permute-start.65
  313.8 3.9 collective-permute-start.69
  320.7 4.5 collective-permute-start.71
  336.1 3.9 collective-permute-start.75
  343.0 4.5 collective-permute-start.77
  359.1 3.9 collective-permute-start.81
  366.0 4.8 collective-permute-start.83
  384.1 3.9 collective-permute-start.87
  391.0 4.5 collective-permute-start.89
  413.7 3.9 collective-permute-start.93
  420.6 4.5 collective-permute-start.95
  428.2 42.7 %all-reduce.155 = (f32[]{:T(128)}, f32[]{:T(128)}) all-reduce(f32[]{:T(128)} %get-tuple-element.11, f32[]{:T(128)} %get-tuple-element.10), channel_id=1, replica_groups=mesh['gx'=4,'gy'=4,'gz'=2] {'gx','gy','gz'}, use_global_device_ids=true, to_apply=%region_10.11 | all-reduce | flops 2 | bytes 16 | tf_op jit(solution)/shard_map/psum | solution.py:250
  (746 shorter events, 253.1 us)
Async XLA Ops:
  3.1 54.8 %collective-permute-start.6 = (f32[1,5,257]{2,1,0:T(8,128)S(1)}, f32[1,5,257]{2,1,0:T(8,128)S(1)}, u32[]{:S(2)}, u32[]{:S(2)}) collective-permute-start(f32[1,5,257]{2,1,0:T(8,128)S(1)} %get-tuple-element.233), channel_id=1, source_target_pairs={{0,8},{8,16},{16,24},{1,9},{9,17},{17,25},{2,10},{10,18},{18,26},{... | collective-permute-start | bytes 15428 | tf_op jit(solution)/shard_map/ppermute | solution.py:20
  5.1 52.9 %collective-permute-start.7 = (f32[1,5,257]{2,1,0:T(8,128)S(1)}, f32[1,5,257]{2,1,0:T(8,128)S(1)}, u32[]{:S(2)}, u32[]{:S(2)}) collective-permute-start(f32[1,5,257]{2,1,0:T(8,128)S(1)} %get-tuple-element.234), channel_id=1, source_target_pairs={{8,0},{16,8},{24,16},{9,1},{17,9},{25,17},{10,2},{18,10},{26,18},{... | collective-permute-start | bytes 15428 | tf_op jit(solution)/shard_map/ppermute | solution.py:22
  9.2 16.8 %collective-permute-start.18 = (f32[1,3,129]{2,1,0:T(4,128)S(1)}, f32[1,3,129]{2,1,0:T(4,128)S(1)}, u32[]{:S(2)}, u32[]{:S(2)}) collective-permute-start(f32[1,3,129]{2,1,0:T(4,128)S(1)} %get-tuple-element.387), channel_id=1, source_target_pairs={{0,8},{8,16},{16,24},{1,9},{9,17},{17,25},{2,10},{10,18},{18,26},{... | collective-permute-start | bytes 4652 | tf_op jit(solution)/shard_map/ppermute | solution.py:20
  11.5 10.1 %collective-permute-start.30 = (f32[1,2,65]{2,1,0:T(2,128)S(1)}, f32[1,2,65]{2,1,0:T(2,128)S(1)}, u32[]{:S(2)}, u32[]{:S(2)}) collective-permute-start(f32[1,2,65]{2,1,0:T(2,128)S(1)} %get-tuple-element.509), channel_id=1, source_target_pairs={{0,8},{8,16},{16,24},{1,9},{9,17},{17,25},{2,10},{10,18},{18,26},{... | collective-permute-start | bytes 1568 | tf_op jit(solution)/shard_map/ppermute | solution.py:20
  13.4 10.6 %collective-permute-start.31 = (f32[1,2,65]{2,1,0:T(2,128)S(1)}, f32[1,2,65]{2,1,0:T(2,128)S(1)}, u32[]{:S(2)}, u32[]{:S(2)}) collective-permute-start(f32[1,2,65]{2,1,0:T(2,128)S(1)} %get-tuple-element.510), channel_id=1, source_target_pairs={{8,0},{16,8},{24,16},{9,1},{17,9},{25,17},{10,2},{18,10},{26,18},{... | collective-permute-start | bytes 1568 | tf_op jit(solution)/shard_map/ppermute | solution.py:22
  21.6 7.9 %collective-permute-start.19 = (f32[1,3,129]{2,1,0:T(4,128)S(1)}, f32[1,3,129]{2,1,0:T(4,128)S(1)}, u32[]{:S(2)}, u32[]{:S(2)}) collective-permute-start(f32[1,3,129]{2,1,0:T(4,128)S(1)} %get-tuple-element.388), channel_id=1, source_target_pairs={{8,0},{16,8},{24,16},{9,1},{17,9},{25,17},{10,2},{18,10},{26,18},{... | collective-permute-start | bytes 4652 | tf_op jit(solution)/shard_map/ppermute | solution.py:22
  24.0 39.8 %collective-permute-start = (f32[1,5,257]{2,1,0:T(8,128)S(1)}, f32[1,5,257]{2,1,0:T(8,128)S(1)}, u32[]{:S(2)}, u32[]{:S(2)}) collective-permute-start(f32[1,5,257]{2,1,0:T(8,128)S(1)} %get-tuple-element.131), channel_id=1, source_target_pairs={{0,8},{8,16},{16,24},{1,9},{9,17},{17,25},{2,10},{10,18},{18,26},{... | collective-permute-start | bytes 15428 | tf_op jit(solution)/shard_map/ppermute | solution.py:20
  36.4 8.1 %collective-permute-start.35 = (f32[4,4,1]{2,1,0:T(4,128)S(1)}, f32[4,4,1]{2,1,0:T(4,128)S(1)}, u32[]{:S(2)}, u32[]{:S(2)}) collective-permute-start(f32[4,4,1]{2,1,0:T(4,128)S(1)} %get-tuple-element.412), channel_id=1, source_target_pairs={{1,0},{3,2},{5,4},{7,6},{9,8},{11,10},{13,12},{15,14},{17,16},{19,... | collective-permute-start | bytes 200 | tf_op jit(solution)/shard_map/ppermute | solution.py:22
  40.9 6.0 %collective-permute-start.20 = (f32[5,1,129]{2,1,0:T(1,128)S(1)}, f32[5,1,129]{2,1,0:T(1,128)S(1)}, u32[]{:S(2)}, u32[]{:S(2)}) collective-permute-start(f32[5,1,129]{2,1,0:T(1,128)S(1)} %get-tuple-element.289), channel_id=1, source_target_pairs={{0,2},{2,4},{4,6},{1,3},{3,5},{5,7},{8,10},{10,12},{12,14},{9,11},... | collective-permute-start | bytes 7748 | tf_op jit(solution)/shard_map/ppermute | solution.py:20
  51.3 6.5 %collective-permute-start.23 = (f32[5,5,1]{2,1,0:T(8,128)S(1)}, f32[5,5,1]{2,1,0:T(8,128)S(1)}, u32[]{:S(2)}, u32[]{:S(2)}) collective-permute-start(f32[5,5,1]{2,1,0:T(8,128)S(1)} %get-tuple-element.258), channel_id=1, source_target_pairs={{1,0},{3,2},{5,4},{7,6},{9,8},{11,10},{13,12},{15,14},{17,16},{19,... | collective-permute-start | bytes 308 | tf_op jit(solution)/shard_map/ppermute | solution.py:22
  55.8 8.0 %collective-permute-start.1 = (f32[1,5,257]{2,1,0:T(8,128)S(1)}, f32[1,5,257]{2,1,0:T(8,128)S(1)}, u32[]{:S(2)}, u32[]{:S(2)}) collective-permute-start(f32[1,5,257]{2,1,0:T(8,128)S(1)} %get-tuple-element.132), channel_id=1, source_target_pairs={{8,0},{16,8},{24,16},{9,1},{17,9},{25,17},{10,2},{18,10},{26,18},{... | collective-permute-start | bytes 15428 | tf_op jit(solution)/shard_map/ppermute | solution.py:22
  58.0 11.8 %collective-permute-start.8 = (f32[7,1,257]{2,1,0:T(1,128)S(1)}, f32[7,1,257]{2,1,0:T(1,128)S(1)}, u32[]{:S(2)}, u32[]{:S(2)}) collective-permute-start(f32[7,1,257]{2,1,0:T(1,128)S(1)} %get-tuple-element.143), channel_id=1, source_target_pairs={{0,2},{2,4},{4,6},{1,3},{3,5},{5,7},{8,10},{10,12},{12,14},{9,11},... | collective-permute-start | bytes 21596 | tf_op jit(solution)/shard_map/ppermute | solution.py:20
  59.9 9.8 %collective-permute-start.9 = (f32[7,1,257]{2,1,0:T(1,128)S(1)}, f32[7,1,257]{2,1,0:T(1,128)S(1)}, u32[]{:S(2)}, u32[]{:S(2)}) collective-permute-start(f32[7,1,257]{2,1,0:T(1,128)S(1)} %get-tuple-element.144), channel_id=1, source_target_pairs={{2,0},{4,2},{6,4},{3,1},{5,3},{7,5},{10,8},{12,10},{14,12},{11,9},... | collective-permute-start | bytes 21596 | tf_op jit(solution)/shard_map/ppermute | solution.py:22
  63.9 11.8 %collective-permute-start.2 = (f32[7,1,257]{2,1,0:T(1,128)S(1)}, f32[7,1,257]{2,1,0:T(1,128)S(1)}, u32[]{:S(2)}, u32[]{:S(2)}) collective-permute-start(f32[7,1,257]{2,1,0:T(1,128)S(1)} %get-tuple-element.141), channel_id=1, source_target_pairs={{0,2},{2,4},{4,6},{1,3},{3,5},{5,7},{8,10},{10,12},{12,14},{9,11},... | collective-permute-start | bytes 21596 | tf_op jit(solution)/shard_map/ppermute | solution.py:20
  65.8 9.8 %collective-permute-start.3 = (f32[7,1,257]{2,1,0:T(1,128)S(1)}, f32[7,1,257]{2,1,0:T(1,128)S(1)}, u32[]{:S(2)}, u32[]{:S(2)}) collective-permute-start(f32[7,1,257]{2,1,0:T(1,128)S(1)} %get-tuple-element.142), channel_id=1, source_target_pairs={{2,0},{4,2},{6,4},{3,1},{5,3},{7,5},{10,8},{12,10},{14,12},{11,9},... | collective-permute-start | bytes 21596 | tf_op jit(solution)/shard_map/ppermute | solution.py:22
  69.8 11.8 %collective-permute-start.10 = (f32[7,7,1]{2,1,0:T(8,128)S(1)}, f32[7,7,1]{2,1,0:T(8,128)S(1)}, u32[]{:S(2)}, u32[]{:S(2)}) collective-permute-start(f32[7,7,1]{2,1,0:T(8,128)S(1)} %get-tuple-element.125), channel_id=1, source_target_pairs={{0,1},{2,3},{4,5},{6,7},{8,9},{10,11},{12,13},{14,15},{16,17},{18,... | collective-permute-start | bytes 596 | tf_op jit(solution)/shard_map/ppermute | solution.py:20
  71.1 10.5 %collective-permute-start.11 = (f32[7,7,1]{2,1,0:T(8,128)S(1)}, f32[7,7,1]{2,1,0:T(8,128)S(1)}, u32[]{:S(2)}, u32[]{:S(2)}) collective-permute-start(f32[7,7,1]{2,1,0:T(8,128)S(1)} %get-tuple-element.126), channel_id=1, source_target_pairs={{1,0},{3,2},{5,4},{7,6},{9,8},{11,10},{13,12},{15,14},{17,16},{19,... | collective-permute-start | bytes 596 | tf_op jit(solution)/shard_map/ppermute | solution.py:22
  75.7 6.3 %collective-permute-start.4 = (f32[7,7,1]{2,1,0:T(8,128)S(1)}, f32[7,7,1]{2,1,0:T(8,128)S(1)}, u32[]{:S(2)}, u32[]{:S(2)}) collective-permute-start(f32[7,7,1]{2,1,0:T(8,128)S(1)} %get-tuple-element.123), channel_id=1, source_target_pairs={{0,1},{2,3},{4,5},{6,7},{8,9},{10,11},{12,13},{14,15},{16,17},{18,... | collective-permute-start | bytes 596 | tf_op jit(solution)/shard_map/ppermute | solution.py:20
  77.0 6.1 %collective-permute-start.5 = (f32[7,7,1]{2,1,0:T(8,128)S(1)}, f32[7,7,1]{2,1,0:T(8,128)S(1)}, u32[]{:S(2)}, u32[]{:S(2)}) collective-permute-start(f32[7,7,1]{2,1,0:T(8,128)S(1)} %get-tuple-element.124), channel_id=1, source_target_pairs={{1,0},{3,2},{5,4},{7,6},{9,8},{11,10},{13,12},{15,14},{17,16},{19,... | collective-permute-start | bytes 596 | tf_op jit(solution)/shard_map/ppermute | solution.py:22
  94.5 5.9 %collective-permute-start.14 = (f32[5,1,129]{2,1,0:T(1,128)S(1)}, f32[5,1,129]{2,1,0:T(1,128)S(1)}, u32[]{:S(2)}, u32[]{:S(2)}) collective-permute-start(f32[5,1,129]{2,1,0:T(1,128)S(1)} %get-tuple-element.291), channel_id=1, source_target_pairs={{0,2},{2,4},{4,6},{1,3},{3,5},{5,7},{8,10},{10,12},{12,14},{9,11},... | collective-permute-start | bytes 7748 | tf_op jit(solution)/shard_map/ppermute | solution.py:20
  102.0 5.9 %collective-permute-start.16 = (f32[5,5,1]{2,1,0:T(8,128)S(1)}, f32[5,5,1]{2,1,0:T(8,128)S(1)}, u32[]{:S(2)}, u32[]{:S(2)}) collective-permute-start(f32[5,5,1]{2,1,0:T(8,128)S(1)} %get-tuple-element.262), channel_id=1, source_target_pairs={{0,1},{2,3},{4,5},{6,7},{8,9},{10,11},{12,13},{14,15},{16,17},{18,... | collective-permute-start | bytes 308 | tf_op jit(solution)/shard_map/ppermute | solution.py:20
  103.3 6.0 %collective-permute-start.17 = (f32[5,5,1]{2,1,0:T(8,128)S(1)}, f32[5,5,1]{2,1,0:T(8,128)S(1)}, u32[]{:S(2)}, u32[]{:S(2)}) collective-permute-start(f32[5,5,1]{2,1,0:T(8,128)S(1)} %get-tuple-element.263), channel_id=1, source_target_pairs={{1,0},{3,2},{5,4},{7,6},{9,8},{11,10},{13,12},{15,14},{17,16},{19,... | collective-permute-start | bytes 308 | tf_op jit(solution)/shard_map/ppermute | solution.py:22
  117.4 6.0 %collective-permute-start.26 = (f32[4,1,65]{2,1,0:T(1,128)S(1)}, f32[4,1,65]{2,1,0:T(1,128)S(1)}, u32[]{:S(2)}, u32[]{:S(2)}) collective-permute-start(f32[4,1,65]{2,1,0:T(1,128)S(1)} %get-tuple-element.472), channel_id=1, source_target_pairs={{0,2},{2,4},{4,6},{1,3},{3,5},{5,7},{8,10},{10,12},{12,14},{9,11},... | collective-permute-start | bytes 3128 | tf_op jit(solution)/shard_map/ppermute | solution.py:20
  148.5 5.9 %collective-permute-start.41 = (f32[4,4,1]{2,1,0:T(4,128)S(1)}, f32[4,4,1]{2,1,0:T(4,128)S(1)}, u32[]{:S(2)}, u32[]{:S(2)}) collective-permute-start(f32[4,4,1]{2,1,0:T(4,128)S(1)} %get-tuple-element.408), channel_id=1, source_target_pairs={{1,0},{3,2},{5,4},{7,6},{9,8},{11,10},{13,12},{15,14},{17,16},{19,... | collective-permute-start | bytes 200 | tf_op jit(solution)/shard_map/ppermute | solution.py:22
  171.4 6.0 %collective-permute-start.47 = (f32[5,5,1]{2,1,0:T(8,128)S(1)}, f32[5,5,1]{2,1,0:T(8,128)S(1)}, u32[]{:S(2)}, u32[]{:S(2)}) collective-permute-start(f32[5,5,1]{2,1,0:T(8,128)S(1)} %get-tuple-element.253), channel_id=1, source_target_pairs={{1,0},{3,2},{5,4},{7,6},{9,8},{11,10},{13,12},{15,14},{17,16},{19,... | collective-permute-start | bytes 308 | tf_op jit(solution)/shard_map/ppermute | solution.py:22
  197.8 6.1 %collective-permute-start.53 = (f32[7,7,1]{2,1,0:T(8,128)S(1)}, f32[7,7,1]{2,1,0:T(8,128)S(1)}, u32[]{:S(2)}, u32[]{:S(2)}) collective-permute-start(f32[7,7,1]{2,1,0:T(8,128)S(1)} %get-tuple-element.122), channel_id=1, source_target_pairs={{1,0},{3,2},{5,4},{7,6},{9,8},{11,10},{13,12},{15,14},{17,16},{19,... | collective-permute-start | bytes 596 | tf_op jit(solution)/shard_map/ppermute | solution.py:22
  228.1 6.1 %collective-permute-start.59 = (f32[7,7,1]{2,1,0:T(8,128)S(1)}, f32[7,7,1]{2,1,0:T(8,128)S(1)}, u32[]{:S(2)}, u32[]{:S(2)}) collective-permute-start(f32[7,7,1]{2,1,0:T(8,128)S(1)} %get-tuple-element.120), channel_id=1, source_target_pairs={{1,0},{3,2},{5,4},{7,6},{9,8},{11,10},{13,12},{15,14},{17,16},{19,... | collective-permute-start | bytes 596 | tf_op jit(solution)/shard_map/ppermute | solution.py:22
  297.8 6.0 %collective-permute-start.65 = (f32[5,5,1]{2,1,0:T(8,128)S(1)}, f32[5,5,1]{2,1,0:T(8,128)S(1)}, u32[]{:S(2)}, u32[]{:S(2)}) collective-permute-start(f32[5,5,1]{2,1,0:T(8,128)S(1)} %get-tuple-element.246), channel_id=1, source_target_pairs={{1,0},{3,2},{5,4},{7,6},{9,8},{11,10},{13,12},{15,14},{17,16},{19,... | collective-permute-start | bytes 308 | tf_op jit(solution)/shard_map/ppermute | solution.py:22
  364.7 6.1 %collective-permute-start.82 = (f32[5,5,1]{2,1,0:T(8,128)S(1)}, f32[5,5,1]{2,1,0:T(8,128)S(1)}, u32[]{:S(2)}, u32[]{:S(2)}) collective-permute-start(f32[5,5,1]{2,1,0:T(8,128)S(1)} %get-tuple-element.240), channel_id=1, source_target_pairs={{0,1},{2,3},{4,5},{6,7},{8,9},{10,11},{12,13},{14,15},{16,17},{18,... | collective-permute-start | bytes 308 | tf_op jit(solution)/shard_map/ppermute | solution.py:20
  366.0 6.0 %collective-permute-start.83 = (f32[5,5,1]{2,1,0:T(8,128)S(1)}, f32[5,5,1]{2,1,0:T(8,128)S(1)}, u32[]{:S(2)}, u32[]{:S(2)}) collective-permute-start(f32[5,5,1]{2,1,0:T(8,128)S(1)} %get-tuple-element.241), channel_id=1, source_target_pairs={{1,0},{3,2},{5,4},{7,6},{9,8},{11,10},{13,12},{15,14},{17,16},{19,... | collective-permute-start | bytes 308 | tf_op jit(solution)/shard_map/ppermute | solution.py:22
  391.0 6.1 %collective-permute-start.89 = (f32[7,7,1]{2,1,0:T(8,128)S(1)}, f32[7,7,1]{2,1,0:T(8,128)S(1)}, u32[]{:S(2)}, u32[]{:S(2)}) collective-permute-start(f32[7,7,1]{2,1,0:T(8,128)S(1)} %get-tuple-element.118), channel_id=1, source_target_pairs={{1,0},{3,2},{5,4},{7,6},{9,8},{11,10},{13,12},{15,14},{17,16},{19,... | collective-permute-start | bytes 596 | tf_op jit(solution)/shard_map/ppermute | solution.py:22
  420.6 6.1 %collective-permute-start.95 = (f32[7,7,1]{2,1,0:T(8,128)S(1)}, f32[7,7,1]{2,1,0:T(8,128)S(1)}, u32[]{:S(2)}, u32[]{:S(2)}) collective-permute-start(f32[7,7,1]{2,1,0:T(8,128)S(1)} %get-tuple-element.116), channel_id=1, source_target_pairs={{1,0},{3,2},{5,4},{7,6},{9,8},{11,10},{13,12},{15,14},{17,16},{19,... | collective-permute-start | bytes 596 | tf_op jit(solution)/shard_map/ppermute | solution.py:22
  (85 other events, 377.1 us)
where the time goes:
time: 480 us; the launch traced here: 477 us
  starting transfers between devices  273 us (57%)
  blocking collectives  85.4 us (18%)
  waiting for transfers between devices  59.4 us (12%)
  local copies, waits for them, and re-layouts  27.5 us (6%)
  other arithmetic  17.6 us (4%)
  between operations  10.7 us (2%)
    ppermute x48, starting transfers between devices, extended(): lax.ppermute(head, axis, [((i + 1) % count, i) for i in range(ends)])  187 us
    ppermute x48, starting transfers between devices, extended(): lax.ppermute(tail, axis, [(i, (i + 1) % count) for i in range(ends)])  85.8 us
    psum x2, blocking collectives, inner_pair(): return lax.psum((local_rho, local_curv), ('gx', 'gy', 'gz'))  85.4 us
    ppermute x48, waiting for transfers between devices, extended(): lax.ppermute(head, axis, [((i + 1) % count, i) for i in range(ends)])  59.3 us
  transfers between devices with their start and end apart: 96, of which 39 were waited for; matrix products, arithmetic and copies ran while one was open for 1% of the time, Pallas kernels for 0%

commit v1 on v0

--- a/solution.py
+++ b/solution.py
@@ -247,7 +247,7 @@
 def inner_pair(resid, precond, image):
     local_rho = jnp.sum(resid[1:, 1:, 1:] * precond[1:, 1:, 1:])
     local_curv = jnp.sum(precond[1:, 1:, 1:] * image[1:, 1:, 1:])
-    return lax.psum((local_rho, local_curv), ("gx", "gy", "gz"))
+    return lax.psum(lax.psum((local_rho, local_curv), ("gy", "gz")), "gx")
 
 
 def body(kappa, source):

time: 480 us -> 450 us (0.938)
  blocking collectives: 85.4 us -> 50.5 us
    psum x2 -> x4, blocking collectives: 85.4 us -> 50.5 us  [inner_pair(): return lax.psum(lax.psum((local_rho, local_curv), ('gy', 'gz')), 'gx')]
where the time goes in v1:
time: 450 us; the launch traced here: 444 us
  starting transfers between devices  274 us (61%)
  waiting for transfers between devices  61.1 us (14%)
  blocking collectives  50.5 us (11%)
  local copies, waits for them, and re-layouts  27.5 us (6%)
  other arithmetic  17.6 us (4%)
  between operations  10.8 us (2%)
    ppermute x48, starting transfers between devices, extended(): lax.ppermute(head, axis, [((i + 1) % count, i) for i in range(ends)])  187 us
    ppermute x48, starting transfers between devices, extended(): lax.ppermute(tail, axis, [(i, (i + 1) % count) for i in range(ends)])  87.2 us
    ppermute x48, waiting for transfers between devices, extended(): lax.ppermute(head, axis, [((i + 1) % count, i) for i in range(ends)])  61 us
    psum x4, blocking collectives, inner_pair(): return lax.psum(lax.psum((local_rho, local_curv), ('gy', 'gz')), 'gx')  50.5 us
  transfers between devices with their start and end apart: 96, of which 39 were waited for; matrix products, arithmetic and copies ran while one was open for 1% of the time, Pallas kernels for 0%

profile of v1, /device:TPU:14, one launch (start us, length us, event | category | flops | bytes accessed | tf_op | source)
XLA Modules:
  0.0 444.3 jit_solution(137154279380583342)
XLA Ops:
  36.4 4.5 %collective-permute-start.35 = (f32[4,4,1]{2,1,0:T(4,128)S(1)}, f32[4,4,1]{2,1,0:T(4,128)S(1)}, u32[]{:S(2)}, u32[]{:S(2)}) collective-permute-start(f32[4,4,1]{2,1,0:T(4,128)S(1)} %get-tuple-element.416), channel_id=1, source_target_pairs={{1,0},{3,2},{5,4},{7,6},{9,8},{11,10},{13,12},{15,14},{17,16},{19,... | collective-permute-start | bytes 200 | tf_op jit(solution)/shard_map/ppermute | solution.py:22
  51.3 4.5 %collective-permute-start.23 = (f32[5,5,1]{2,1,0:T(8,128)S(1)}, f32[5,5,1]{2,1,0:T(8,128)S(1)}, u32[]{:S(2)}, u32[]{:S(2)}) collective-permute-start(f32[5,5,1]{2,1,0:T(8,128)S(1)} %get-tuple-element.262), channel_id=1, source_target_pairs={{1,0},{3,2},{5,4},{7,6},{9,8},{11,10},{13,12},{15,14},{17,16},{19,... | collective-permute-start | bytes 308 | tf_op jit(solution)/shard_map/ppermute | solution.py:22
  59.9 3.9 collective-permute-start.9
  71.1 4.5 %collective-permute-start.11 = (f32[7,7,1]{2,1,0:T(8,128)S(1)}, f32[7,7,1]{2,1,0:T(8,128)S(1)}, u32[]{:S(2)}, u32[]{:S(2)}) collective-permute-start(f32[7,7,1]{2,1,0:T(8,128)S(1)} %get-tuple-element.130), channel_id=1, source_target_pairs={{1,0},{3,2},{5,4},{7,6},{9,8},{11,10},{13,12},{15,14},{17,16},{19,... | collective-permute-start | bytes 596 | tf_op jit(solution)/shard_map/ppermute | solution.py:22
  77.0 4.5 %collective-permute-start.5 = (f32[7,7,1]{2,1,0:T(8,128)S(1)}, f32[7,7,1]{2,1,0:T(8,128)S(1)}, u32[]{:S(2)}, u32[]{:S(2)}) collective-permute-start(f32[7,7,1]{2,1,0:T(8,128)S(1)} %get-tuple-element.128), channel_id=1, source_target_pairs={{1,0},{3,2},{5,4},{7,6},{9,8},{11,10},{13,12},{15,14},{17,16},{19,... | collective-permute-start | bytes 596 | tf_op jit(solution)/shard_map/ppermute | solution.py:22
  103.3 4.5 %collective-permute-start.17 = (f32[5,5,1]{2,1,0:T(8,128)S(1)}, f32[5,5,1]{2,1,0:T(8,128)S(1)}, u32[]{:S(2)}, u32[]{:S(2)}) collective-permute-start(f32[5,5,1]{2,1,0:T(8,128)S(1)} %get-tuple-element.267), channel_id=1, source_target_pairs={{1,0},{3,2},{5,4},{7,6},{9,8},{11,10},{13,12},{15,14},{17,16},{19,... | collective-permute-start | bytes 308 | tf_op jit(solution)/shard_map/ppermute | solution.py:22
  119.3 3.9 collective-permute-start.27
  126.2 4.5 %collective-permute-start.29 = (f32[4,4,1]{2,1,0:T(4,128)S(1)}, f32[4,4,1]{2,1,0:T(4,128)S(1)}, u32[]{:S(2)}, u32[]{:S(2)}) collective-permute-start(f32[4,4,1]{2,1,0:T(4,128)S(1)} %get-tuple-element.420), channel_id=1, source_target_pairs={{1,0},{3,2},{5,4},{7,6},{9,8},{11,10},{13,12},{15,14},{17,16},{19,... | collective-permute-start | bytes 200 | tf_op jit(solution)/shard_map/ppermute | solution.py:22
  141.6 3.9 collective-permute-start.39
  148.5 4.5 %collective-permute-start.41 = (f32[4,4,1]{2,1,0:T(4,128)S(1)}, f32[4,4,1]{2,1,0:T(4,128)S(1)}, u32[]{:S(2)}, u32[]{:S(2)}) collective-permute-start(f32[4,4,1]{2,1,0:T(4,128)S(1)} %get-tuple-element.412), channel_id=1, source_target_pairs={{1,0},{3,2},{5,4},{7,6},{9,8},{11,10},{13,12},{15,14},{17,16},{19,... | collective-permute-start | bytes 200 | tf_op jit(solution)/shard_map/ppermute | solution.py:22
  164.6 3.9 collective-permute-start.45
  171.4 4.5 %collective-permute-start.47 = (f32[5,5,1]{2,1,0:T(8,128)S(1)}, f32[5,5,1]{2,1,0:T(8,128)S(1)}, u32[]{:S(2)}, u32[]{:S(2)}) collective-permute-start(f32[5,5,1]{2,1,0:T(8,128)S(1)} %get-tuple-element.257), channel_id=1, source_target_pairs={{1,0},{3,2},{5,4},{7,6},{9,8},{11,10},{13,12},{15,14},{17,16},{19,... | collective-permute-start | bytes 308 | tf_op jit(solution)/shard_map/ppermute | solution.py:22
  190.9 3.9 collective-permute-start.51
  197.8 4.5 %collective-permute-start.53 = (f32[7,7,1]{2,1,0:T(8,128)S(1)}, f32[7,7,1]{2,1,0:T(8,128)S(1)}, u32[]{:S(2)}, u32[]{:S(2)}) collective-permute-start(f32[7,7,1]{2,1,0:T(8,128)S(1)} %get-tuple-element.126), channel_id=1, source_target_pairs={{1,0},{3,2},{5,4},{7,6},{9,8},{11,10},{13,12},{15,14},{17,16},{19,... | collective-permute-start | bytes 596 | tf_op jit(solution)/shard_map/ppermute | solution.py:22
  221.2 3.9 collective-permute-start.57
  228.1 4.5 %collective-permute-start.59 = (f32[7,7,1]{2,1,0:T(8,128)S(1)}, f32[7,7,1]{2,1,0:T(8,128)S(1)}, u32[]{:S(2)}, u32[]{:S(2)}) collective-permute-start(f32[7,7,1]{2,1,0:T(8,128)S(1)} %get-tuple-element.124), channel_id=1, source_target_pairs={{1,0},{3,2},{5,4},{7,6},{9,8},{11,10},{13,12},{15,14},{17,16},{19,... | collective-permute-start | bytes 596 | tf_op jit(solution)/shard_map/ppermute | solution.py:22
  235.6 18.8 %all-reduce.156 = (f32[]{:T(128)}, f32[]{:T(128)}) all-reduce(f32[]{:T(128)} %get-tuple-element.13, f32[]{:T(128)} %get-tuple-element.12), channel_id=1, replica_groups=mesh['gx'=4,'gy'=4,'gz'=2] {'gy','gz'}, use_global_device_ids=true, to_apply=%region_6.7 | all-reduce | flops 2 | bytes 16 | tf_op jit(solution)/shard_map/psum | solution.py:250
  254.4 6.4 %all-reduce.158 = (f32[]{:T(128)}, f32[]{:T(128)}) all-reduce(f32[]{:T(128)} %get-tuple-element.16, f32[]{:T(128)} %get-tuple-element.17), channel_id=1, replica_groups=mesh['gx'=4,'gy'=4,'gz'=2] {'gx'}, use_global_device_ids=true, to_apply=%region_7.8 | all-reduce | flops 2 | bytes 16 | tf_op jit(solution)/shard_map/psum | solution.py:250
  272.8 4.5 %collective-permute-start.63 = (f32[5,1,129]{2,1,0:T(1,128)S(1)}, f32[5,1,129]{2,1,0:T(1,128)S(1)}, u32[]{:S(2)}, u32[]{:S(2)}) collective-permute-start(f32[5,1,129]{2,1,0:T(1,128)S(1)} %get-tuple-element.288), channel_id=1, source_target_pairs={{2,0},{4,2},{6,4},{3,1},{5,3},{7,5},{10,8},{12,10},{14,12},{11,9},... | collective-permute-start | bytes 7748 | tf_op jit(solution)/shard_map/ppermute | solution.py:22
  280.5 4.5 %collective-permute-start.65 = (f32[5,5,1]{2,1,0:T(8,128)S(1)}, f32[5,5,1]{2,1,0:T(8,128)S(1)}, u32[]{:S(2)}, u32[]{:S(2)}) collective-permute-start(f32[5,5,1]{2,1,0:T(8,128)S(1)} %get-tuple-element.250), channel_id=1, source_target_pairs={{1,0},{3,2},{5,4},{7,6},{9,8},{11,10},{13,12},{15,14},{17,16},{19,... | collective-permute-start | bytes 308 | tf_op jit(solution)/shard_map/ppermute | solution.py:22
  294.7 3.9 collective-permute-start.68
  305.5 4.5 %collective-permute-start.71 = (f32[4,4,1]{2,1,0:T(4,128)S(1)}, f32[4,4,1]{2,1,0:T(4,128)S(1)}, u32[]{:S(2)}, u32[]{:S(2)}) collective-permute-start(f32[4,4,1]{2,1,0:T(4,128)S(1)} %get-tuple-element.408), channel_id=1, source_target_pairs={{1,0},{3,2},{5,4},{7,6},{9,8},{11,10},{13,12},{15,14},{17,16},{19,... | collective-permute-start | bytes 200 | tf_op jit(solution)/shard_map/ppermute | solution.py:22
  320.9 3.9 collective-permute-start.75
  327.8 4.5 %collective-permute-start.77 = (f32[4,4,1]{2,1,0:T(4,128)S(1)}, f32[4,4,1]{2,1,0:T(4,128)S(1)}, u32[]{:S(2)}, u32[]{:S(2)}) collective-permute-start(f32[4,4,1]{2,1,0:T(4,128)S(1)} %get-tuple-element.404), channel_id=1, source_target_pairs={{1,0},{3,2},{5,4},{7,6},{9,8},{11,10},{13,12},{15,14},{17,16},{19,... | collective-permute-start | bytes 200 | tf_op jit(solution)/shard_map/ppermute | solution.py:22
  343.9 3.9 collective-permute-start.81
  350.7 4.5 %collective-permute-start.83 = (f32[5,5,1]{2,1,0:T(8,128)S(1)}, f32[5,5,1]{2,1,0:T(8,128)S(1)}, u32[]{:S(2)}, u32[]{:S(2)}) collective-permute-start(f32[5,5,1]{2,1,0:T(8,128)S(1)} %get-tuple-element.245), channel_id=1, source_target_pairs={{1,0},{3,2},{5,4},{7,6},{9,8},{11,10},{13,12},{15,14},{17,16},{19,... | collective-permute-start | bytes 308 | tf_op jit(solution)/shard_map/ppermute | solution.py:22
  368.8 3.9 collective-permute-start.87
  375.7 4.8 %collective-permute-start.89 = (f32[7,7,1]{2,1,0:T(8,128)S(1)}, f32[7,7,1]{2,1,0:T(8,128)S(1)}, u32[]{:S(2)}, u32[]{:S(2)}) collective-permute-start(f32[7,7,1]{2,1,0:T(8,128)S(1)} %get-tuple-element.122), channel_id=1, source_target_pairs={{1,0},{3,2},{5,4},{7,6},{9,8},{11,10},{13,12},{15,14},{17,16},{19,... | collective-permute-start | bytes 596 | tf_op jit(solution)/shard_map/ppermute | solution.py:22
  398.5 3.9 collective-permute-start.93
  405.4 4.5 %collective-permute-start.95 = (f32[7,7,1]{2,1,0:T(8,128)S(1)}, f32[7,7,1]{2,1,0:T(8,128)S(1)}, u32[]{:S(2)}, u32[]{:S(2)}) collective-permute-start(f32[7,7,1]{2,1,0:T(8,128)S(1)} %get-tuple-element.120), channel_id=1, source_target_pairs={{1,0},{3,2},{5,4},{7,6},{9,8},{11,10},{13,12},{15,14},{17,16},{19,... | collective-permute-start | bytes 596 | tf_op jit(solution)/shard_map/ppermute | solution.py:22
  412.9 18.9 %all-reduce.155 = (f32[]{:T(128)}, f32[]{:T(128)}) all-reduce(f32[]{:T(128)} %get-tuple-element.11, f32[]{:T(128)} %get-tuple-element.10), channel_id=1, replica_groups=mesh['gx'=4,'gy'=4,'gz'=2] {'gy','gz'}, use_global_device_ids=true, to_apply=%region_12.13 | all-reduce | flops 2 | bytes 16 | tf_op jit(solution)/shard_map/psum | solution.py:250
  431.8 6.4 %all-reduce.157 = (f32[]{:T(128)}, f32[]{:T(128)}) all-reduce(f32[]{:T(128)} %get-tuple-element.14, f32[]{:T(128)} %get-tuple-element.15), channel_id=1, replica_groups=mesh['gx'=4,'gy'=4,'gz'=2] {'gx'}, use_global_device_ids=true, to_apply=%region_13.14 | all-reduce | flops 2 | bytes 16 | tf_op jit(solution)/shard_map/psum | solution.py:250
  (748 shorter events, 262.5 us)
Async XLA Ops:
  3.1 54.8 %collective-permute-start.6 = (f32[1,5,257]{2,1,0:T(8,128)S(1)}, f32[1,5,257]{2,1,0:T(8,128)S(1)}, u32[]{:S(2)}, u32[]{:S(2)}) collective-permute-start(f32[1,5,257]{2,1,0:T(8,128)S(1)} %get-tuple-element.237), channel_id=1, source_target_pairs={{0,8},{8,16},{16,24},{1,9},{9,17},{17,25},{2,10},{10,18},{18,26},{... | collective-permute-start | bytes 15428 | tf_op jit(solution)/shard_map/ppermute | solution.py:20
  5.1 52.9 %collective-permute-start.7 = (f32[1,5,257]{2,1,0:T(8,128)S(1)}, f32[1,5,257]{2,1,0:T(8,128)S(1)}, u32[]{:S(2)}, u32[]{:S(2)}) collective-permute-start(f32[1,5,257]{2,1,0:T(8,128)S(1)} %get-tuple-element.238), channel_id=1, source_target_pairs={{8,0},{16,8},{24,16},{9,1},{17,9},{25,17},{10,2},{18,10},{26,18},{... | collective-permute-start | bytes 15428 | tf_op jit(solution)/shard_map/ppermute | solution.py:22
  9.2 16.8 %collective-permute-start.18 = (f32[1,3,129]{2,1,0:T(4,128)S(1)}, f32[1,3,129]{2,1,0:T(4,128)S(1)}, u32[]{:S(2)}, u32[]{:S(2)}) collective-permute-start(f32[1,3,129]{2,1,0:T(4,128)S(1)} %get-tuple-element.391), channel_id=1, source_target_pairs={{0,8},{8,16},{16,24},{1,9},{9,17},{17,25},{2,10},{10,18},{18,26},{... | collective-permute-start | bytes 4652 | tf_op jit(solution)/shard_map/ppermute | solution.py:20
  11.5 10.1 %collective-permute-start.30 = (f32[1,2,65]{2,1,0:T(2,128)S(1)}, f32[1,2,65]{2,1,0:T(2,128)S(1)}, u32[]{:S(2)}, u32[]{:S(2)}) collective-permute-start(f32[1,2,65]{2,1,0:T(2,128)S(1)} %get-tuple-element.513), channel_id=1, source_target_pairs={{0,8},{8,16},{16,24},{1,9},{9,17},{17,25},{2,10},{10,18},{18,26},{... | collective-permute-start | bytes 1568 | tf_op jit(solution)/shard_map/ppermute | solution.py:20
  13.4 10.6 %collective-permute-start.31 = (f32[1,2,65]{2,1,0:T(2,128)S(1)}, f32[1,2,65]{2,1,0:T(2,128)S(1)}, u32[]{:S(2)}, u32[]{:S(2)}) collective-permute-start(f32[1,2,65]{2,1,0:T(2,128)S(1)} %get-tuple-element.514), channel_id=1, source_target_pairs={{8,0},{16,8},{24,16},{9,1},{17,9},{25,17},{10,2},{18,10},{26,18},{... | collective-permute-start | bytes 1568 | tf_op jit(solution)/shard_map/ppermute | solution.py:22
  21.6 7.9 %collective-permute-start.19 = (f32[1,3,129]{2,1,0:T(4,128)S(1)}, f32[1,3,129]{2,1,0:T(4,128)S(1)}, u32[]{:S(2)}, u32[]{:S(2)}) collective-permute-start(f32[1,3,129]{2,1,0:T(4,128)S(1)} %get-tuple-element.392), channel_id=1, source_target_pairs={{8,0},{16,8},{24,16},{9,1},{17,9},{25,17},{10,2},{18,10},{26,18},{... | collective-permute-start | bytes 4652 | tf_op jit(solution)/shard_map/ppermute | solution.py:22
  24.0 39.8 %collective-permute-start = (f32[1,5,257]{2,1,0:T(8,128)S(1)}, f32[1,5,257]{2,1,0:T(8,128)S(1)}, u32[]{:S(2)}, u32[]{:S(2)}) collective-permute-start(f32[1,5,257]{2,1,0:T(8,128)S(1)} %get-tuple-element.135), channel_id=1, source_target_pairs={{0,8},{8,16},{16,24},{1,9},{9,17},{17,25},{2,10},{10,18},{18,26},{... | collective-permute-start | bytes 15428 | tf_op jit(solution)/shard_map/ppermute | solution.py:20
  36.4 8.1 %collective-permute-start.35 = (f32[4,4,1]{2,1,0:T(4,128)S(1)}, f32[4,4,1]{2,1,0:T(4,128)S(1)}, u32[]{:S(2)}, u32[]{:S(2)}) collective-permute-start(f32[4,4,1]{2,1,0:T(4,128)S(1)} %get-tuple-element.416), channel_id=1, source_target_pairs={{1,0},{3,2},{5,4},{7,6},{9,8},{11,10},{13,12},{15,14},{17,16},{19,... | collective-permute-start | bytes 200 | tf_op jit(solution)/shard_map/ppermute | solution.py:22
  40.9 6.0 %collective-permute-start.20 = (f32[5,1,129]{2,1,0:T(1,128)S(1)}, f32[5,1,129]{2,1,0:T(1,128)S(1)}, u32[]{:S(2)}, u32[]{:S(2)}) collective-permute-start(f32[5,1,129]{2,1,0:T(1,128)S(1)} %get-tuple-element.293), channel_id=1, source_target_pairs={{0,2},{2,4},{4,6},{1,3},{3,5},{5,7},{8,10},{10,12},{12,14},{9,11},... | collective-permute-start | bytes 7748 | tf_op jit(solution)/shard_map/ppermute | solution.py:20
  51.3 6.5 %collective-permute-start.23 = (f32[5,5,1]{2,1,0:T(8,128)S(1)}, f32[5,5,1]{2,1,0:T(8,128)S(1)}, u32[]{:S(2)}, u32[]{:S(2)}) collective-permute-start(f32[5,5,1]{2,1,0:T(8,128)S(1)} %get-tuple-element.262), channel_id=1, source_target_pairs={{1,0},{3,2},{5,4},{7,6},{9,8},{11,10},{13,12},{15,14},{17,16},{19,... | collective-permute-start | bytes 308 | tf_op jit(solution)/shard_map/ppermute | solution.py:22
  55.8 8.0 %collective-permute-start.1 = (f32[1,5,257]{2,1,0:T(8,128)S(1)}, f32[1,5,257]{2,1,0:T(8,128)S(1)}, u32[]{:S(2)}, u32[]{:S(2)}) collective-permute-start(f32[1,5,257]{2,1,0:T(8,128)S(1)} %get-tuple-element.136), channel_id=1, source_target_pairs={{8,0},{16,8},{24,16},{9,1},{17,9},{25,17},{10,2},{18,10},{26,18},{... | collective-permute-start | bytes 15428 | tf_op jit(solution)/shard_map/ppermute | solution.py:22
  58.0 11.8 %collective-permute-start.8 = (f32[7,1,257]{2,1,0:T(1,128)S(1)}, f32[7,1,257]{2,1,0:T(1,128)S(1)}, u32[]{:S(2)}, u32[]{:S(2)}) collective-permute-start(f32[7,1,257]{2,1,0:T(1,128)S(1)} %get-tuple-element.147), channel_id=1, source_target_pairs={{0,2},{2,4},{4,6},{1,3},{3,5},{5,7},{8,10},{10,12},{12,14},{9,11},... | collective-permute-start | bytes 21596 | tf_op jit(solution)/shard_map/ppermute | solution.py:20
  59.9 9.8 %collective-permute-start.9 = (f32[7,1,257]{2,1,0:T(1,128)S(1)}, f32[7,1,257]{2,1,0:T(1,128)S(1)}, u32[]{:S(2)}, u32[]{:S(2)}) collective-permute-start(f32[7,1,257]{2,1,0:T(1,128)S(1)} %get-tuple-element.148), channel_id=1, source_target_pairs={{2,0},{4,2},{6,4},{3,1},{5,3},{7,5},{10,8},{12,10},{14,12},{11,9},... | collective-permute-start | bytes 21596 | tf_op jit(solution)/shard_map/ppermute | solution.py:22
  63.9 11.8 %collective-permute-start.2 = (f32[7,1,257]{2,1,0:T(1,128)S(1)}, f32[7,1,257]{2,1,0:T(1,128)S(1)}, u32[]{:S(2)}, u32[]{:S(2)}) collective-permute-start(f32[7,1,257]{2,1,0:T(1,128)S(1)} %get-tuple-element.145), channel_id=1, source_target_pairs={{0,2},{2,4},{4,6},{1,3},{3,5},{5,7},{8,10},{10,12},{12,14},{9,11},... | collective-permute-start | bytes 21596 | tf_op jit(solution)/shard_map/ppermute | solution.py:20
  65.8 9.8 %collective-permute-start.3 = (f32[7,1,257]{2,1,0:T(1,128)S(1)}, f32[7,1,257]{2,1,0:T(1,128)S(1)}, u32[]{:S(2)}, u32[]{:S(2)}) collective-permute-start(f32[7,1,257]{2,1,0:T(1,128)S(1)} %get-tuple-element.146), channel_id=1, source_target_pairs={{2,0},{4,2},{6,4},{3,1},{5,3},{7,5},{10,8},{12,10},{14,12},{11,9},... | collective-permute-start | bytes 21596 | tf_op jit(solution)/shard_map/ppermute | solution.py:22
  69.8 11.8 %collective-permute-start.10 = (f32[7,7,1]{2,1,0:T(8,128)S(1)}, f32[7,7,1]{2,1,0:T(8,128)S(1)}, u32[]{:S(2)}, u32[]{:S(2)}) collective-permute-start(f32[7,7,1]{2,1,0:T(8,128)S(1)} %get-tuple-element.129), channel_id=1, source_target_pairs={{0,1},{2,3},{4,5},{6,7},{8,9},{10,11},{12,13},{14,15},{16,17},{18,... | collective-permute-start | bytes 596 | tf_op jit(solution)/shard_map/ppermute | solution.py:20
  71.1 10.5 %collective-permute-start.11 = (f32[7,7,1]{2,1,0:T(8,128)S(1)}, f32[7,7,1]{2,1,0:T(8,128)S(1)}, u32[]{:S(2)}, u32[]{:S(2)}) collective-permute-start(f32[7,7,1]{2,1,0:T(8,128)S(1)} %get-tuple-element.130), channel_id=1, source_target_pairs={{1,0},{3,2},{5,4},{7,6},{9,8},{11,10},{13,12},{15,14},{17,16},{19,... | collective-permute-start | bytes 596 | tf_op jit(solution)/shard_map/ppermute | solution.py:22
  75.7 6.3 %collective-permute-start.4 = (f32[7,7,1]{2,1,0:T(8,128)S(1)}, f32[7,7,1]{2,1,0:T(8,128)S(1)}, u32[]{:S(2)}, u32[]{:S(2)}) collective-permute-start(f32[7,7,1]{2,1,0:T(8,128)S(1)} %get-tuple-element.127), channel_id=1, source_target_pairs={{0,1},{2,3},{4,5},{6,7},{8,9},{10,11},{12,13},{14,15},{16,17},{18,... | collective-permute-start | bytes 596 | tf_op jit(solution)/shard_map/ppermute | solution.py:20
  77.0 6.1 %collective-permute-start.5 = (f32[7,7,1]{2,1,0:T(8,128)S(1)}, f32[7,7,1]{2,1,0:T(8,128)S(1)}, u32[]{:S(2)}, u32[]{:S(2)}) collective-permute-start(f32[7,7,1]{2,1,0:T(8,128)S(1)} %get-tuple-element.128), channel_id=1, source_target_pairs={{1,0},{3,2},{5,4},{7,6},{9,8},{11,10},{13,12},{15,14},{17,16},{19,... | collective-permute-start | bytes 596 | tf_op jit(solution)/shard_map/ppermute | solution.py:22
  94.5 5.9 %collective-permute-start.14 = (f32[5,1,129]{2,1,0:T(1,128)S(1)}, f32[5,1,129]{2,1,0:T(1,128)S(1)}, u32[]{:S(2)}, u32[]{:S(2)}) collective-permute-start(f32[5,1,129]{2,1,0:T(1,128)S(1)} %get-tuple-element.295), channel_id=1, source_target_pairs={{0,2},{2,4},{4,6},{1,3},{3,5},{5,7},{8,10},{10,12},{12,14},{9,11},... | collective-permute-start | bytes 7748 | tf_op jit(solution)/shard_map/ppermute | solution.py:20
  103.3 6.0 %collective-permute-start.17 = (f32[5,5,1]{2,1,0:T(8,128)S(1)}, f32[5,5,1]{2,1,0:T(8,128)S(1)}, u32[]{:S(2)}, u32[]{:S(2)}) collective-permute-start(f32[5,5,1]{2,1,0:T(8,128)S(1)} %get-tuple-element.267), channel_id=1, source_target_pairs={{1,0},{3,2},{5,4},{7,6},{9,8},{11,10},{13,12},{15,14},{17,16},{19,... | collective-permute-start | bytes 308 | tf_op jit(solution)/shard_map/ppermute | solution.py:22
  117.4 6.0 %collective-permute-start.26 = (f32[4,1,65]{2,1,0:T(1,128)S(1)}, f32[4,1,65]{2,1,0:T(1,128)S(1)}, u32[]{:S(2)}, u32[]{:S(2)}) collective-permute-start(f32[4,1,65]{2,1,0:T(1,128)S(1)} %get-tuple-element.476), channel_id=1, source_target_pairs={{0,2},{2,4},{4,6},{1,3},{3,5},{5,7},{8,10},{10,12},{12,14},{9,11},... | collective-permute-start | bytes 3128 | tf_op jit(solution)/shard_map/ppermute | solution.py:20
  171.4 6.0 %collective-permute-start.47 = (f32[5,5,1]{2,1,0:T(8,128)S(1)}, f32[5,5,1]{2,1,0:T(8,128)S(1)}, u32[]{:S(2)}, u32[]{:S(2)}) collective-permute-start(f32[5,5,1]{2,1,0:T(8,128)S(1)} %get-tuple-element.257), channel_id=1, source_target_pairs={{1,0},{3,2},{5,4},{7,6},{9,8},{11,10},{13,12},{15,14},{17,16},{19,... | collective-permute-start | bytes 308 | tf_op jit(solution)/shard_map/ppermute | solution.py:22
  197.8 6.1 %collective-permute-start.53 = (f32[7,7,1]{2,1,0:T(8,128)S(1)}, f32[7,7,1]{2,1,0:T(8,128)S(1)}, u32[]{:S(2)}, u32[]{:S(2)}) collective-permute-start(f32[7,7,1]{2,1,0:T(8,128)S(1)} %get-tuple-element.126), channel_id=1, source_target_pairs={{1,0},{3,2},{5,4},{7,6},{9,8},{11,10},{13,12},{15,14},{17,16},{19,... | collective-permute-start | bytes 596 | tf_op jit(solution)/shard_map/ppermute | solution.py:22
  228.1 6.1 %collective-permute-start.59 = (f32[7,7,1]{2,1,0:T(8,128)S(1)}, f32[7,7,1]{2,1,0:T(8,128)S(1)}, u32[]{:S(2)}, u32[]{:S(2)}) collective-permute-start(f32[7,7,1]{2,1,0:T(8,128)S(1)} %get-tuple-element.124), channel_id=1, source_target_pairs={{1,0},{3,2},{5,4},{7,6},{9,8},{11,10},{13,12},{15,14},{17,16},{19,... | collective-permute-start | bytes 596 | tf_op jit(solution)/shard_map/ppermute | solution.py:22
  270.9 6.5 %collective-permute-start.62 = (f32[5,1,129]{2,1,0:T(1,128)S(1)}, f32[5,1,129]{2,1,0:T(1,128)S(1)}, u32[]{:S(2)}, u32[]{:S(2)}) collective-permute-start(f32[5,1,129]{2,1,0:T(1,128)S(1)} %get-tuple-element.287), channel_id=1, source_target_pairs={{0,2},{2,4},{4,6},{1,3},{3,5},{5,7},{8,10},{10,12},{12,14},{9,11},... | collective-permute-start | bytes 7748 | tf_op jit(solution)/shard_map/ppermute | solution.py:20
  272.8 6.4 %collective-permute-start.63 = (f32[5,1,129]{2,1,0:T(1,128)S(1)}, f32[5,1,129]{2,1,0:T(1,128)S(1)}, u32[]{:S(2)}, u32[]{:S(2)}) collective-permute-start(f32[5,1,129]{2,1,0:T(1,128)S(1)} %get-tuple-element.288), channel_id=1, source_target_pairs={{2,0},{4,2},{6,4},{3,1},{5,3},{7,5},{10,8},{12,10},{14,12},{11,9},... | collective-permute-start | bytes 7748 | tf_op jit(solution)/shard_map/ppermute | solution.py:22
  280.5 6.0 %collective-permute-start.65 = (f32[5,5,1]{2,1,0:T(8,128)S(1)}, f32[5,5,1]{2,1,0:T(8,128)S(1)}, u32[]{:S(2)}, u32[]{:S(2)}) collective-permute-start(f32[5,5,1]{2,1,0:T(8,128)S(1)} %get-tuple-element.250), channel_id=1, source_target_pairs={{1,0},{3,2},{5,4},{7,6},{9,8},{11,10},{13,12},{15,14},{17,16},{19,... | collective-permute-start | bytes 308 | tf_op jit(solution)/shard_map/ppermute | solution.py:22
  350.7 6.0 %collective-permute-start.83 = (f32[5,5,1]{2,1,0:T(8,128)S(1)}, f32[5,5,1]{2,1,0:T(8,128)S(1)}, u32[]{:S(2)}, u32[]{:S(2)}) collective-permute-start(f32[5,5,1]{2,1,0:T(8,128)S(1)} %get-tuple-element.245), channel_id=1, source_target_pairs={{1,0},{3,2},{5,4},{7,6},{9,8},{11,10},{13,12},{15,14},{17,16},{19,... | collective-permute-start | bytes 308 | tf_op jit(solution)/shard_map/ppermute | solution.py:22
  374.4 6.1 %collective-permute-start.88 = (f32[7,7,1]{2,1,0:T(8,128)S(1)}, f32[7,7,1]{2,1,0:T(8,128)S(1)}, u32[]{:S(2)}, u32[]{:S(2)}) collective-permute-start(f32[7,7,1]{2,1,0:T(8,128)S(1)} %get-tuple-element.121), channel_id=1, source_target_pairs={{0,1},{2,3},{4,5},{6,7},{8,9},{10,11},{12,13},{14,15},{16,17},{18,... | collective-permute-start | bytes 596 | tf_op jit(solution)/shard_map/ppermute | solution.py:20
  375.7 6.1 %collective-permute-start.89 = (f32[7,7,1]{2,1,0:T(8,128)S(1)}, f32[7,7,1]{2,1,0:T(8,128)S(1)}, u32[]{:S(2)}, u32[]{:S(2)}) collective-permute-start(f32[7,7,1]{2,1,0:T(8,128)S(1)} %get-tuple-element.122), channel_id=1, source_target_pairs={{1,0},{3,2},{5,4},{7,6},{9,8},{11,10},{13,12},{15,14},{17,16},{19,... | collective-permute-start | bytes 596 | tf_op jit(solution)/shard_map/ppermute | solution.py:22
  405.4 6.1 %collective-permute-start.95 = (f32[7,7,1]{2,1,0:T(8,128)S(1)}, f32[7,7,1]{2,1,0:T(8,128)S(1)}, u32[]{:S(2)}, u32[]{:S(2)}) collective-permute-start(f32[7,7,1]{2,1,0:T(8,128)S(1)} %get-tuple-element.120), channel_id=1, source_target_pairs={{1,0},{3,2},{5,4},{7,6},{9,8},{11,10},{13,12},{15,14},{17,16},{19,... | collective-permute-start | bytes 596 | tf_op jit(solution)/shard_map/ppermute | solution.py:22
  (85 other events, 377.6 us)
